TPU v7x, 32 devices: a whole 2x2x4 slice. The times are simulated.
32 devices in a mesh: seq: 16 (over z, y, core), mp: 2 (over x).
Axes of the slice: x: 2, y: 2, z: 4, core: 2. Of those that a mesh axis runs over, the one named last changes fastest.
Arguments:
- stream: bfloat16 [2048, 8192], P('seq', 'mp'), may hold values from -17 to 17
- norm_gain: float32 [8192], P('mp'), may hold values from 0.5 to 1.5
- short_outer: bfloat16 [2048, 8192], P('seq', 'mp'), may hold values from -4 to 4
- short_inner: bfloat16 [2048, 8192], P('seq', 'mp'), may hold values from -4 to 4
- short_filter: bfloat16 [128, 8192], P(None, 'mp'), may hold values from -0.5 to 0.5
- long_outer: bfloat16 [2048, 8192], P('seq', 'mp'), may hold values from -4 to 4
- long_inner: bfloat16 [2048, 8192], P('seq', 'mp'), may hold values from -4 to 4
- long_decay: float32 [8192], P('mp'), may hold values from 1e-06 to 0.03
- query_heads: bfloat16 [2048, 8192], P('seq', 'mp'), may hold values from -6 to 6
- key_heads: bfloat16 [2048, 8192], P('seq', 'mp'), may hold values from -6 to 6
Outputs:
- long_mixed: bfloat16 [2048, 8192], P('seq', 'mp')
- attended: bfloat16 [2048, 8192], P('seq', 'mp')
All inputs are finite; a program needn't handle non-finite values.
Results may differ from a plain program's by a relative error of at most 0.013.
Values may be sent and summed in bfloat16 or wider, within the bound.
A program may use at most 64 MiB of HBM per device.

v0:
```python
import jax
import jax.numpy as jnp
from jax import lax
from jax.sharding import PartitionSpec as P

D = 8192
HEAD_DIM = 128


def shifted(block, axis, distance):
    devices = range(lax.axis_size(axis))
    route = [(i - distance, i) for i in devices if i - distance in devices]
    return lax.ppermute(block, axis, route)


def carried_in(part, axis, combine, identity):
    place = lax.axis_index(axis)
    gathered = jax.tree.map(lambda a: lax.all_gather(a, axis), part)
    state = jax.tree.map(lambda a, e: jnp.zeros_like(a) + jnp.asarray(e, a.dtype), part, identity)

    def one(turn, state):
        return combine(
            state, jax.tree.map(lambda a: lax.dynamic_index_in_dim(a, turn, 0, False), gathered)
        )

    return lax.fori_loop(0, place, one, state)


def pair_combine(first_pair, second_pair):
    return (first_pair[0] * second_pair[0], second_pair[0] * first_pair[1] + second_pair[1])


def on_device(
    stream,
    norm_gain,
    short_outer,
    short_inner,
    short_filter,
    long_outer,
    long_inner,
    long_decay,
    query_heads,
    key_heads,
):
    rows_here = stream.shape[0]
    width_here = stream.shape[1]
    x_float = stream.astype(jnp.float32)
    totals = lax.psum(jnp.sum(x_float * x_float, axis=1), "mp")
    normed = x_float * norm_gain / jnp.sqrt(totals[:, None] / D + 0.5)
    short_in = (short_inner.astype(jnp.float32) * normed).astype(jnp.bfloat16)
    filter_len = short_filter.shape[0]
    tail_rows = shifted(short_in[rows_here - (filter_len - 1) :], "seq", 1)
    extended = jnp.concatenate([tail_rows, short_in], axis=0).astype(jnp.float32)
    kernel = short_filter.astype(jnp.float32)[::-1][:, None, :]
    short_conv = lax.conv_general_dilated(
        extended[None],
        kernel,
        (1,),
        [(0, 0)],
        dimension_numbers=("NWC", "WIO", "NWC"),
        feature_group_count=width_here,
        precision=lax.Precision.HIGHEST,
    )[0]
    long_in = (
        long_inner.astype(jnp.float32) * short_outer.astype(jnp.float32) * short_conv
    ).astype(jnp.bfloat16)
    rates = jnp.exp(-long_decay)
    scales = jnp.sqrt(-jnp.expm1(-2.0 * long_decay))
    factors = jnp.broadcast_to(rates, long_in.shape)
    powers, states = lax.associative_scan(
        pair_combine, (factors, long_in.astype(jnp.float32)), axis=0
    )
    identity = (jnp.ones((width_here,), jnp.float32), jnp.zeros((width_here,), jnp.float32))
    carried = carried_in((powers[-1], states[-1]), "seq", pair_combine, identity)
    long_conv = (states + powers * carried[1]) * scales
    long_mixed = (long_outer.astype(jnp.float32) * long_conv).astype(jnp.bfloat16)
    stacked = jnp.stack([key_heads, long_mixed])
    before = shifted(stacked, "seq", 1)
    heads_here = width_here // HEAD_DIM
    keys = jnp.concatenate([before[0], key_heads], axis=0).reshape(
        2 * rows_here, heads_here, HEAD_DIM
    )
    values = jnp.concatenate([before[1], long_mixed], axis=0).reshape(
        2 * rows_here, heads_here, HEAD_DIM
    )
    query = query_heads.reshape(rows_here, heads_here, HEAD_DIM)
    scores = jnp.einsum(
        "thd,shd->hts", query, keys, preferred_element_type=jnp.float32
    ) * HEAD_DIM ** (-0.5)
    row_pos = jnp.arange(rows_here, dtype=jnp.int32)[:, None]
    col_pos = jnp.arange(2 * rows_here, dtype=jnp.int32)[None, :]
    valid = (col_pos <= row_pos + rows_here) & (
        (col_pos >= rows_here) | (lax.axis_index("seq") > 0)
    )
    scores = jnp.where(valid[None], scores, -1e30)
    weights = jax.nn.softmax(scores, axis=-1).astype(jnp.bfloat16)
    result = jnp.einsum("hts,shd->thd", weights, values, preferred_element_type=jnp.float32)
    attended = result.reshape(rows_here, width_here).astype(jnp.bfloat16)
    return (long_mixed, attended)


def solution(mesh):
    return jax.shard_map(
        on_device,
        mesh=mesh,
        in_specs=(
            P("seq", "mp"),
            P("mp"),
            P("seq", "mp"),
            P("seq", "mp"),
            P(None, "mp"),
            P("seq", "mp"),
            P("seq", "mp"),
            P("mp"),
            P("seq", "mp"),
            P("seq", "mp"),
        ),
        out_specs=(P("seq", "mp"), P("seq", "mp")),
        check_vma=False,
    )
```

profile of v0, /device:TPU:1, one launch (start us, length us, event | category | flops | bytes accessed | tf_op | source)
XLA Modules:
  0.0 247.8 jit_solution(3769319546112353525)
XLA Ops:
  2.3 4.3 %psum.7 = f32[128]{0:T(128)S(1)} all-reduce(f32[128]{0:T(128)S(1)} %fusion.7), channel_id=1, replica_groups=mesh['seq'=16,'mp'=2] {'mp'}, use_global_device_ids=true, to_apply=%region_1.0 | all-reduce | flops 128 | bytes 1024 | tf_op jit(solution)/shard_map/psum | solution.py:48
  9.9 5.2 %collective-permute-start = (bf16[127,4096]{1,0:T(8,128)(2,1)}, bf16[127,4096]{1,0:T(8,128)(2,1)}, u32[]{:S(2)}, u32[]{:S(2)}) collective-permute-start(bf16[127,4096]{1,0:T(8,128)(2,1)} %slice.257), channel_id=1, source_target_pairs={{0,2},{2,4},{4,6},{6,8},{8,10},{10,12},{12,14},{14,16},{16,18},{18... | collective-permute-start | bytes 3121160 | tf_op jit(solution)/shard_map/ppermute | solution.py:13
  15.2 10.6 %rev.3 = f32[128,4096]{1,0:T(8,128)} reverse(bf16[128,4096]{1,0:T(8,128)(2,1)S(1)} %copy-done.11), dimensions={0} | reverse | bytes 3145728 | tf_op jit(solution)/shard_map/rev | solution.py:54
  29.7 23.8 %fusion.1 = f32[1,128,4096]{2,0,1:T(1,128)S(1)} fusion(bf16[1,255,4096]{2,1,0:T(8,128)(2,1)S(1)} %maximum_bitcast_fusion, f32[128,1,4096]{2,0,1:T(8,128)S(1)} %bitcast.67), kind=kOutput, calls=%fused_computation.7 | convolution fusion | flops 805306368 | bytes 6283264 | tf_op jit(solution)/shard_map/conv_general_dilated | solution.py:55
  55.4 3.0 %slice.200 = f32[64,4096]{1,0:T(8,128)} slice(f32[128,4096]{1,0:T(8,128)S(1)} %fusion.24), slice={[0:127:2], [0:4096:1]} | slice | bytes 2097152 | tf_op jit(solution)/shard_map/slice | solution.py:70
  58.4 2.8 %slice.201 = f32[64,4096]{1,0:T(8,128)} slice(f32[128,4096]{1,0:T(8,128)S(1)} %fusion.24), slice={[1:128:2], [0:4096:1]} | slice | bytes 2097152 | tf_op jit(solution)/shard_map/slice | solution.py:70
  61.2 2.6 %multiply_add_fusion.1 = f32[64,4096]{1,0:T(8,128)} fusion(f32[64,4096]{1,0:T(8,128)} %slice.201, f32[64,4096]{1,0:T(8,128)} %slice.200, f32[4096]{0:T(1024)S(1)} %get-tuple-element.80), kind=kLoop, calls=%fused_computation.43 | loop fusion | flops 524288 | bytes 3162112 | tf_op jit(solution)/shard_map/add | solution.py:30
  63.8 3.3 %slice.205 = f32[32,4096]{1,0:T(8,128)} slice(f32[64,4096]{1,0:T(8,128)} %multiply_add_fusion.1), slice={[0:63:2], [0:4096:1]} | slice | bytes 1048576 | tf_op jit(solution)/shard_map/slice | solution.py:70
  67.1 3.3 %slice.206 = f32[32,4096]{1,0:T(8,128)} slice(f32[64,4096]{1,0:T(8,128)} %multiply_add_fusion.1), slice={[1:64:2], [0:4096:1]} | slice | bytes 1048576 | tf_op jit(solution)/shard_map/slice | solution.py:70
  88.2 3.3 %slice.239 = f32[31,4096]{1,0:T(8,128)} slice(f32[64,4096]{1,0:T(8,128)} %multiply_add_fusion.1), slice={[2:64:2], [0:4096:1]} | slice | bytes 1015808 | tf_op jit(solution)/shard_map/slice | solution.py:70
  91.5 3.0 %slice.241 = f32[63,4096]{1,0:T(8,128)} slice(f32[128,4096]{1,0:T(8,128)S(1)} %fusion.24), slice={[2:128:2], [0:4096:1]} | slice | bytes 2064384 | tf_op jit(solution)/shard_map/slice | solution.py:70
  112.4 8.6 %pad.100 = f32[128,4096]{1,0:T(8,128)} pad(f32[64,4096]{1,0:T(8,128)} %add.193, f32[]{:T(128)} %constant.17.clone.1), padding=1_0_1x0_0_0 | pad | bytes 3145732 | tf_op jit(solution)/shard_map/pad | solution.py:70
  121.0 4.6 %pad.112 = f32[64,4096]{1,0:T(8,128)} pad(f32[32,4096]{1,0:T(8,128)} %add.200, f32[]{:T(128)} %constant.17.clone.1), padding=1_0_1x0_0_0 | pad | bytes 1572868 | tf_op jit(solution)/shard_map/pad | solution.py:70
  127.5 4.7 %pad.111 = f32[64,4096]{1,0:T(8,128)} pad(f32[32,4096]{1,0:T(8,128)} %pad_maximum_fusion.4, f32[]{:T(128)} %constant.17.clone.1), padding=0_1_1x0_0_0 | pad | bytes 1572868 | tf_op jit(solution)/shard_map/pad | solution.py:70
  132.2 2.8 %add.201 = f32[64,4096]{1,0:T(8,128)} add(f32[64,4096]{1,0:T(8,128)} %pad.111, f32[64,4096]{1,0:T(8,128)} %pad.112) | non-fusion elementwise | flops 262144 | bytes 3145728 | tf_op jit(solution)/shard_map/add | solution.py:70
  137.5 4.2 %pad.99 = f32[128,4096]{1,0:T(8,128)S(1)} pad(f32[64,4096]{1,0:T(8,128)} %pad_maximum_fusion.1, f32[]{:T(128)} %constant.17.clone.1), padding=0_1_1x0_0_0 | pad | bytes 3145732 | tf_op jit(solution)/shard_map/pad | solution.py:70
  142.7 22.7 %all-gather.1 = f32[16,1,4096]{2,1,0:T(1,128)S(1)} all-gather(f32[1,1,4096]{2,1,0:T(1,128)S(1)} %add_bitcast_fusion), channel_id=1, replica_groups=mesh['seq'=16,'mp'=2] {'seq'}, dimensions={0}, use_global_device_ids=true | all-gather | bytes 278528 | tf_op jit(solution)/shard_map/all_gather | solution.py:18
  165.6 8.7 %pad.114 = f32[128,4096]{1,0:T(8,128)} pad(f32[64,4096]{1,0:T(8,128)} %add.201, f32[]{:T(128)} %constant.17.clone.1), padding=1_0_1x0_0_0 | pad | bytes 3145732 | tf_op jit(solution)/shard_map/pad | solution.py:70
  176.5 8.7 %pad.113 = f32[128,4096]{1,0:T(8,128)} pad(f32[64,4096]{1,0:T(8,128)} %pad_maximum_fusion.2, f32[]{:T(128)} %constant.17.clone.1), padding=0_1_1x0_0_0 | pad | bytes 3145732 | tf_op jit(solution)/shard_map/pad | solution.py:70
  186.3 18.2 %all-gather = f32[16,1,4096]{2,1,0:T(1,128)S(1)} all-gather(f32[1,1,4096]{2,1,0:T(1,128)S(1)} %add_bitcast_fusion.1), channel_id=1, replica_groups=mesh['seq'=16,'mp'=2] {'seq'}, dimensions={0}, use_global_device_ids=true | all-gather | bytes 278528 | tf_op jit(solution)/shard_map/all_gather | solution.py:18
  204.9 4.6 %multiply_convert_fusion = bf16[128,4096]{1,0:T(8,128)(2,1)S(1)} fusion(f32[128,4096]{1,0:T(8,128)} %pad.113, f32[128,4096]{1,0:T(8,128)} %pad.114, f32[128,4096]{1,0:T(8,128)} %copy-done.5, f32[128,4096]{1,0:T(8,128)} %pad.100, bf16[128,4096]{1,0:T(8,128)(2,1)} %param.17, f32[4096]{0:T(1024)S(1)} %copy-done.29, f32[4096]{0:T(1024)S(1)} %get-tuple-element.46), kind=kLoop, calls=%fused_computation.31 | loop fusion | flops 4194304 | bytes 10518528 | tf_op jit(solution)/shard_map/convert_element_type | solution.py:76
  211.2 3.4 %collective-permute-start.1 = (bf16[2,128,4096]{2,1,0:T(8,128)(2,1)}, bf16[2,128,4096]{2,1,0:T(8,128)(2,1)}, u32[]{:S(2)}, u32[]{:S(2)}) collective-permute-start(bf16[2,128,4096]{2,1,0:T(8,128)(2,1)} %pad_maximum_fusion), channel_id=1, source_target_pairs={{0,2},{2,4},{4,6},{6,8},{8,10},{10,12},{12,14},{14,16},{16,18},{18... | collective-permute-start | bytes 6291464 | tf_op jit(solution)/shard_map/ppermute | solution.py:13
  219.1 18.8 %collective-permute-done.1 = bf16[2,128,4096]{2,1,0:T(8,128)(2,1)} collective-permute-done((bf16[2,128,4096]{2,1,0:T(8,128)(2,1)}, bf16[2,128,4096]{2,1,0:T(8,128)(2,1)}, u32[]{:S(2)}, u32[]{:S(2)}) %collective-permute-start.1) | collective-permute-done | bytes 2097184 | tf_op jit(solution)/shard_map/ppermute | solution.py:13
  237.9 2.7 %fusion.45 = (bf16[1,128,4096]{2,1,0:T(8,128)(2,1)}, bf16[16,8,32,128]{3,1,2,0:T(8,128)(2,1)S(1)}) fusion(bf16[2,128,4096]{2,1,0:T(8,128)(2,1)} %collective-permute-done.1), kind=kLoop, calls=%fused_computation.105 | loop fusion | bytes 4194304 | tf_op jit(solution)/shard_map/slice | solution.py:83
  (165 shorter events, 68.7 us)
Async XLA Ops:
  0.6 242.9 %copy-start = (bf16[128,4096]{1,0:T(8,128)(2,1)S(1)}, bf16[128,4096]{1,0:T(8,128)(2,1)}, u32[]{:S(2)}) copy-start(bf16[128,4096]{1,0:T(8,128)(2,1)} %param.20) | copy-start | bytes 3145732
  6.6 8.6 %copy-start.11 = (bf16[128,4096]{1,0:T(8,128)(2,1)S(1)}, bf16[128,4096]{1,0:T(8,128)(2,1)}, u32[]{:S(2)}) copy-start(bf16[128,4096]{1,0:T(8,128)(2,1)} %param.16) | copy-start | bytes 3145732
  9.9 15.9 %copy-start.30 = (f32[4096]{0:T(1024)S(1)}, f32[4096]{0:T(1024)}, u32[]{:S(2)}) copy-start(f32[4096]{0:T(1024)} %param.19) | copy-start | bytes 49156
  9.9 17.9 %collective-permute-start = (bf16[127,4096]{1,0:T(8,128)(2,1)}, bf16[127,4096]{1,0:T(8,128)(2,1)}, u32[]{:S(2)}, u32[]{:S(2)}) collective-permute-start(bf16[127,4096]{1,0:T(8,128)(2,1)} %slice.257), channel_id=1, source_target_pairs={{0,2},{2,4},{4,6},{6,8},{8,10},{10,12},{12,14},{14,16},{16,18},{18... | collective-permute-start | bytes 3121160 | tf_op jit(solution)/shard_map/ppermute | solution.py:13
  26.4 34.8 %copy-start.19 = (f32[4096]{0:T(1024)}, f32[4096]{0:T(1024)S(1)}, u32[]{:S(2)}) copy-start(f32[4096]{0:T(1024)S(1)} %get-tuple-element.80) | copy-start | bytes 49156
  26.4 44.0 %copy-start.21 = (f32[4096]{0:T(1024)}, f32[4096]{0:T(1024)S(1)}, u32[]{:S(2)}) copy-start(f32[4096]{0:T(1024)S(1)} %get-tuple-element.79) | copy-start | bytes 49156
  26.4 49.4 %copy-start.23 = (f32[4096]{0:T(1024)}, f32[4096]{0:T(1024)S(1)}, u32[]{:S(2)}) copy-start(f32[4096]{0:T(1024)S(1)} %get-tuple-element.73) | copy-start | bytes 49156
  26.4 52.0 %copy-start.24 = (f32[4096]{0:T(1024)}, f32[4096]{0:T(1024)S(1)}, u32[]{:S(2)}) copy-start(f32[4096]{0:T(1024)S(1)} %get-tuple-element.74) | copy-start | bytes 49156
  29.7 23.8 %copy-start.15 = (bf16[128,4096]{1,0:T(8,128)(2,1)S(1)}, bf16[128,4096]{1,0:T(8,128)(2,1)}, u32[]{:S(2)}) copy-start(bf16[128,4096]{1,0:T(8,128)(2,1)} %param.14) | copy-start | bytes 3145732
  29.7 23.8 %copy-start.16 = (bf16[128,4096]{1,0:T(8,128)(2,1)S(1)}, bf16[128,4096]{1,0:T(8,128)(2,1)}, u32[]{:S(2)}) copy-start(bf16[128,4096]{1,0:T(8,128)(2,1)} %param.18) | copy-start | bytes 3145732
  55.4 39.1 %copy-start.1 = (f32[128,4096]{1,0:T(8,128)}, f32[128,4096]{1,0:T(8,128)S(1)}, u32[]{:S(2)}) copy-start(f32[128,4096]{1,0:T(8,128)S(1)} %fusion.24) | copy-start | bytes 6291460
  76.9 17.6 %copy-start.10 = (f32[16,4096]{1,0:T(8,128)}, f32[16,4096]{1,0:T(8,128)S(1)}, u32[]{:S(2)}) copy-start(f32[16,4096]{1,0:T(8,128)S(1)} %multiply_add_fusion.3) | copy-start | bytes 786436
  79.4 15.1 %copy-start.17 = (f32[8,4096]{1,0:T(8,128)}, f32[8,4096]{1,0:T(8,128)S(1)}, u32[]{:S(2)}) copy-start(f32[8,4096]{1,0:T(8,128)S(1)} %multiply_add_fusion.4) | copy-start | bytes 393220
  85.8 9.6 %copy-start.27 = (f32[4096]{0:T(1024)S(1)}, f32[4096]{0:T(1024)}, u32[]{:S(2)}) copy-start(f32[4096]{0:T(1024)} %copy-done.26) | copy-start | bytes 49156
  94.5 5.7 %slice-start.4 = ((f32[8,4096]{1,0:T(8,128)}), f32[1,4096]{1,0:T(1,128)S(1)}, s32[]{:S(2)}) async-start(f32[8,4096]{1,0:T(8,128)} %copy-done.17), calls=%async_computation.4 | async-start | bytes 32768 | tf_op jit(solution)/shard_map/slice | solution.py:70
  94.5 5.9 %copy-start.18 = (f32[7,4096]{1,0:T(8,128)S(1)}, f32[7,4096]{1,0:T(8,128)}, u32[]{:S(2)}) copy-start(f32[7,4096]{1,0:T(8,128)} %slice.235) | copy-start | bytes 344068
  94.5 5.9 %copy-start.25 = (f32[4096]{0:T(1024)S(1)}, f32[4096]{0:T(1024)}, u32[]{:S(2)}) copy-start(f32[4096]{0:T(1024)} %copy-done.24) | copy-start | bytes 49156
  101.8 3.4 %slice-start.2 = ((f32[32,4096]{1,0:T(8,128)}), f32[1,4096]{1,0:T(1,128)S(1)}, s32[]{:S(2)}) async-start(f32[32,4096]{1,0:T(8,128)} %multiply_add_fusion.2), calls=%async_computation.2 | async-start | bytes 32768 | tf_op jit(solution)/shard_map/slice | solution.py:70
  127.5 7.5 %copy-start.20 = (f32[4096]{0:T(1024)S(1)}, f32[4096]{0:T(1024)}, u32[]{:S(2)}) copy-start(f32[4096]{0:T(1024)} %copy-done.19) | copy-start | bytes 49156
  141.7 34.9 %copy-start.5 = (f32[128,4096]{1,0:T(8,128)}, f32[128,4096]{1,0:T(8,128)S(1)}, u32[]{:S(2)}) copy-start(f32[128,4096]{1,0:T(8,128)S(1)} %pad.99) | copy-start | bytes 6291460
  176.5 28.3 %copy-start.29 = (f32[4096]{0:T(1024)S(1)}, f32[4096]{0:T(1024)}, u32[]{:S(2)}) copy-start(f32[4096]{0:T(1024)} %get-tuple-element.72) | copy-start | bytes 49156
  204.9 4.6 %copy-start.7 = (bf16[128,4096]{1,0:T(8,128)(2,1)S(1)}, bf16[128,4096]{1,0:T(8,128)(2,1)}, u32[]{:S(2)}) copy-start(bf16[128,4096]{1,0:T(8,128)(2,1)} %param.21) | copy-start | bytes 3145732
  209.5 8.2 %copy-start.4 = (bf16[128,4096]{1,0:T(8,128)(2,1)}, bf16[128,4096]{1,0:T(8,128)(2,1)S(1)}, u32[]{:S(2)}) copy-start(bf16[128,4096]{1,0:T(8,128)(2,1)S(1)} %multiply_convert_fusion) | copy-start | bytes 3145732
  211.2 26.7 %collective-permute-start.1 = (bf16[2,128,4096]{2,1,0:T(8,128)(2,1)}, bf16[2,128,4096]{2,1,0:T(8,128)(2,1)}, u32[]{:S(2)}, u32[]{:S(2)}) collective-permute-start(bf16[2,128,4096]{2,1,0:T(8,128)(2,1)} %pad_maximum_fusion), channel_id=1, source_target_pairs={{0,2},{2,4},{4,6},{6,8},{8,10},{10,12},{12,14},{14,16},{16,18},{18... | collective-permute-start | bytes 6291464 | tf_op jit(solution)/shard_map/ppermute | solution.py:13
  (14 other events, 28.2 us)
where the time goes:
time: 250 us; the launch traced here: 248 us
  local copies, waits for them, and re-layouts  99.9 us (40%)
  other arithmetic  48.5 us (19%)
  blocking collectives  45.2 us (18%)
  matrix products  25.2 us (10%)
  waiting for transfers between devices  18.8 us (8%)
  starting transfers between devices  8.66 us (3%)
    pad x24, local copies, waits for them, and re-layouts, on_device(): lax.associative_scan(pair_combine, (factors, long_in.astype(jnp.float32))...  44.7 us
    all_gather x2, blocking collectives, carried_in(): gathered = jax.tree.map(lambda a: lax.all_gather(a, axis), part)  40.9 us
    slice x27, local copies, waits for them, and re-layouts, on_device(): lax.associative_scan(pair_combine, (factors, long_in.astype(jnp.float32))...  31.1 us
    conv_general_dilated x1, matrix products, on_device(): lax.conv_general_dilated(extended[None], kernel, (1,), [(0, 0)], dimensio...  23.8 us
    ppermute x2, waiting for transfers between devices, shifted(): return lax.ppermute(block, axis, route)  18.8 us
    add x13, other arithmetic, pair_combine(): second_pair[0] * first_pair[1] + second_pair[1]  14 us
    rev x1, local copies, waits for them, and re-layouts, on_device(): kernel = short_filter.astype(jnp.float32)[::-1][:, None, :]  10.6 us
    ppermute x2, starting transfers between devices, shifted(): return lax.ppermute(block, axis, route)  8.66 us
  transfers between devices with their start and end apart: 2, of which 1 were waited for; matrix products, arithmetic and copies ran while one was open for 7% of the time, Pallas kernels for 0%

commit v1 on v0

v1 whole, which is shorter than its diff:
```python
import functools

import jax
import jax.numpy as jnp
import numpy as np
from jax import lax
from jax.experimental import pallas as pl
from jax.experimental.pallas import tpu as pltpu
from jax.sharding import PartitionSpec as P

HEAD_DIM = 128
CHUNKS = 4
TILE = 256
MESH = pl.DeviceIdType.MESH


def dft_matrices(rows):
    size = 2 * rows
    theta = 2.0 * np.pi * (np.arange(rows) + 0.5) / size
    angle = theta[:, None] * np.arange(size)[None, :]
    forward = np.concatenate([np.cos(angle), -np.sin(angle)], axis=0)
    late = angle[:, rows:].T
    inverse = np.concatenate([np.cos(late), -np.sin(late)], axis=1) / rows
    return forward, inverse


def dot(a, b):
    return jnp.dot(a, b, preferred_element_type=jnp.float32)


def kernel(
    n,
    mp,
    channels,
    gain_ref,
    decay_ref,
    stream_hbm,
    souter_hbm,
    sinner_hbm,
    filt_hbm,
    louter_hbm,
    linner_hbm,
    query_hbm,
    key_hbm,
    fwd_hbm,
    inv_hbm,
    mixed_hbm,
    attended_hbm,
    stream,
    souter,
    sinner,
    filt,
    louter,
    linner,
    query,
    fwd,
    inv,
    keys,
    values,
    ext,
    power,
    inv_power,
    cum,
    spectrum,
    weights,
    attended,
    squares,
    squares_in,
    own_state,
    states,
    load_sem,
    key_sem,
    store_sem,
    sq_send,
    sq_recv,
    k_send,
    k_recv,
    t_send,
    t_recv,
    v_send,
    v_recv,
    e_send,
    e_recv,
):
    me = lax.axis_index("seq")
    col = lax.axis_index("mp")
    rows, width = stream.shape
    wide = width // CHUNKS
    tiles = wide // TILE
    heads = wide // HEAD_DIM
    has_next = me < n - 1
    has_prev = me > 0
    own = pl.ds(rows, rows)
    before = pl.ds(0, rows)

    barrier = pltpu.get_barrier_semaphore()

    def greet(k, _):
        pl.semaphore_signal(
            barrier, inc=1, device_id={"seq": lax.rem(me + k, n)}, device_id_type=MESH
        )
        return 0

    lax.fori_loop(1, n, greet, 0)
    for k in range(1, mp):
        pl.semaphore_signal(
            barrier, inc=1, device_id={"mp": lax.rem(col + k, mp)}, device_id_type=MESH
        )

    pairs = [
        (stream_hbm, stream),
        (fwd_hbm, fwd),
        (filt_hbm, filt),
        (sinner_hbm, sinner),
        (inv_hbm, inv),
        (souter_hbm, souter),
        (linner_hbm, linner),
        (louter_hbm, louter),
        (query_hbm, query),
    ]
    loads = [pltpu.make_async_copy(s, d, load_sem.at[i]) for i, (s, d) in enumerate(pairs)]
    key_loads = [
        pltpu.make_async_copy(
            key_hbm.at[:, pl.ds(c * wide, wide)], keys.at[c, own], key_sem.at[c]
        )
        for c in range(CHUNKS)
    ]
    loads[0].start()
    key_loads[0].start()
    for copy in loads[1:]:
        copy.start()
    for copy in key_loads[1:]:
        copy.start()

    def to_next(buffer, c, send, recv):
        return pltpu.make_async_remote_copy(
            src_ref=buffer.at[c, own],
            dst_ref=buffer.at[c, before],
            send_sem=send.at[c],
            recv_sem=recv.at[c],
            device_id={"seq": lax.rem(me + 1, n)},
            device_id_type=MESH,
        )

    k_copies = [to_next(keys, c, k_send, k_recv) for c in range(CHUNKS)]
    t_copies = [to_next(ext, c, t_send, t_recv) for c in range(CHUNKS)]
    v_copies = [to_next(values, c, v_send, v_recv) for c in range(CHUNKS)]

    @pl.when(me == 0)
    def _():
        for c in range(CHUNKS):
            keys[c, :rows, :] = jnp.zeros((rows, wide), keys.dtype)
            values[c, :rows, :] = jnp.zeros((rows, wide), values.dtype)
            ext[c, :rows, :] = jnp.zeros((rows, wide), ext.dtype)

    loads[0].wait()

    def square(i, acc):
        x = stream[:, pl.ds(pl.multiple_of(i * 128, 128), 128)].astype(jnp.float32)
        return acc + x * x

    squares[...] = lax.fori_loop(
        0, width // 128, square, jnp.zeros((rows, 128), jnp.float32), unroll=4
    )
    pl.semaphore_wait(barrier, n - 1 + mp - 1)
    sq_copies = [
        pltpu.make_async_remote_copy(
            src_ref=squares,
            dst_ref=squares_in.at[k - 1],
            send_sem=sq_send.at[k - 1],
            recv_sem=sq_recv.at[k - 1],
            device_id={"mp": lax.rem(col + k, mp)},
            device_id_type=MESH,
        )
        for k in range(1, mp)
    ]
    for copy in sq_copies:
        copy.start()
    key_loads[0].wait()

    @pl.when(has_next)
    def _():
        k_copies[0].start()

    for copy in loads[1:4]:
        copy.wait()

    def spectra(i, _):
        cols = pl.ds(pl.multiple_of(i * TILE, TILE), TILE)
        spectrum[:, cols] = dot(fwd[:, :rows], filt[:, cols])
        return 0

    lax.fori_loop(0, width // TILE, spectra, 0)

    total = squares[...]
    for k, copy in enumerate(sq_copies):
        copy.wait_recv()
        total = total + squares_in[k]
    mean_square = jnp.sum(total, axis=1, keepdims=True) / channels
    norm = 1.0 / jnp.sqrt(mean_square + 0.5)

    for c in range(CHUNKS):

        def short(i, _, c=c):
            cols = pl.ds(pl.multiple_of(c * wide + i * TILE, TILE), TILE)
            x = stream[:, cols].astype(jnp.float32) * gain_ref[:, cols] * norm
            ext[c, own, pl.ds(pl.multiple_of(i * TILE, TILE), TILE)] = (
                sinner[:, cols].astype(jnp.float32) * x
            ).astype(jnp.bfloat16)
            return 0

        lax.fori_loop(0, tiles, short, 0)

        @pl.when(has_next)
        def _(c=c):
            t_copies[c].start()

    step = lax.broadcasted_iota(jnp.int32, (rows, TILE), 0).astype(jnp.float32)

    def powers(i, _):
        cols = pl.ds(pl.multiple_of(i * TILE, TILE), TILE)
        exponent = step * decay_ref[:, cols]
        power[:, cols] = jnp.exp(-exponent)
        inv_power[:, cols] = jnp.exp(exponent)
        return 0

    lax.fori_loop(0, width // TILE, powers, 0)
    for copy in loads[4:]:
        copy.wait()
    row = lax.broadcasted_iota(jnp.int32, (rows, 2 * rows), 0)
    column = lax.broadcasted_iota(jnp.int32, (rows, 2 * rows), 1)
    lower = (jnp.where(column >= rows, column - rows, column) <= row).astype(
        jnp.float32
    ).astype(jnp.bfloat16)

    def state_copy(c, target):
        return pltpu.make_async_remote_copy(
            src_ref=own_state.at[c],
            dst_ref=states.at[c, me],
            send_sem=e_send.at[c, target],
            recv_sem=e_recv.at[c, me],
            device_id={"seq": target},
            device_id_type=MESH,
        )

    for c in range(CHUNKS):

        @pl.when(has_prev)
        def _(c=c):
            t_copies[c].wait_recv()

        def mix(i, _, c=c):
            here = pl.ds(pl.multiple_of(i * TILE, TILE), TILE)
            cols = pl.ds(pl.multiple_of(c * wide + i * TILE, TILE), TILE)
            x = dot(fwd[...], ext[c, :, here])
            x_re, x_im = x[:rows], x[rows:]
            h_re, h_im = spectrum[:rows, cols], spectrum[rows:, cols]
            y = jnp.concatenate(
                [x_re * h_re - x_im * h_im, x_re * h_im + x_im * h_re], axis=0
            ).astype(jnp.bfloat16)
            conv = dot(inv[...], y)
            long_in = (
                linner[:, cols].astype(jnp.float32) * souter[:, cols].astype(jnp.float32) * conv
            ).astype(jnp.bfloat16)
            v = long_in.astype(jnp.float32) * inv_power[:, cols]
            high = v.astype(jnp.bfloat16)
            low = (v - high.astype(jnp.float32)).astype(jnp.bfloat16)
            sums = dot(lower, jnp.concatenate([high, low], axis=0))
            cum[:, cols] = sums
            own_state[c, :, here] = sums[rows - 1 :] * power[rows - 1 :, cols]
            return 0

        lax.fori_loop(0, tiles, mix, 0)

        def send_state(target, _, c=c):
            state_copy(c, target).start()
            return 0

        lax.fori_loop(me + 1, n, send_state, 0)

    for copy in key_loads[1:]:
        copy.wait()

    @pl.when(has_next)
    def _():
        for c in range(1, CHUNKS):
            k_copies[c].start()

    mixed_stores = []
    for c in range(CHUNKS):
        chunk = pl.ds(c * wide, wide)
        rate = decay_ref[:, chunk]
        over_block = jnp.exp(-rate * rows)

        def arrive(j, state, c=c, over_block=over_block):
            pltpu.make_async_remote_copy(
                src_ref=own_state.at[c],
                dst_ref=states.at[c, j],
                send_sem=e_send.at[c, me],
                recv_sem=e_recv.at[c, j],
                device_id={"seq": j},
                device_id_type=MESH,
            ).wait_recv()
            return state * over_block + states[c, j]

        carried = lax.fori_loop(0, me, arrive, jnp.zeros((1, wide), jnp.float32))
        carried = carried * jnp.exp(-rate)
        z = 2.0 * rate
        scale = jnp.sqrt(jnp.tanh(0.5 * z) * (1.0 + jnp.exp(-z)))
        for i in range(tiles):
            here = pl.ds(i * TILE, TILE)
            cols = pl.ds(c * wide + i * TILE, TILE)
            part = slice(i * TILE, (i + 1) * TILE)
            conv = (cum[:, cols] + carried[:, part]) * power[:, cols]
            values[c, own, here] = (
                louter[:, cols].astype(jnp.float32) * (conv * scale[:, part])
            ).astype(jnp.bfloat16)

        @pl.when(has_next)
        def _(c=c):
            v_copies[c].start()

        store = pltpu.make_async_copy(
            values.at[c, own], mixed_hbm.at[:, chunk], store_sem.at[c]
        )
        store.start()
        mixed_stores.append(store)

    valid = (column <= row + rows) & ((column >= rows) | has_prev)
    for c in range(CHUNKS):

        @pl.when(has_prev)
        def _(c=c):
            k_copies[c].wait_recv()

        def score(h, _, c=c):
            here = pl.ds(pl.multiple_of(h * HEAD_DIM, HEAD_DIM), HEAD_DIM)
            cols = pl.ds(pl.multiple_of(c * wide + h * HEAD_DIM, HEAD_DIM), HEAD_DIM)
            s = lax.dot_general(
                query[:, cols],
                keys[c, :, here],
                (((1,), (1,)), ((), ())),
                preferred_element_type=jnp.float32,
            ) * HEAD_DIM ** (-0.5)
            s = jnp.where(valid, s, -1e30)
            e = jnp.exp(s - jnp.max(s, axis=1, keepdims=True))
            e = e * (1.0 / jnp.sum(e, axis=1, keepdims=True))
            weights[c, h] = e.astype(jnp.bfloat16)
            return 0

        lax.fori_loop(0, heads, score, 0, unroll=2)

    out_stores = []
    for c in range(CHUNKS):

        @pl.when(has_prev)
        def _(c=c):
            v_copies[c].wait_recv()

        def gather(h, _, c=c):
            here = pl.ds(pl.multiple_of(h * HEAD_DIM, HEAD_DIM), HEAD_DIM)
            attended[c, :, here] = dot(weights[c, h], values[c, :, here]).astype(jnp.bfloat16)
            return 0

        lax.fori_loop(0, heads, gather, 0, unroll=2)
        store = pltpu.make_async_copy(
            attended.at[c], attended_hbm.at[:, pl.ds(c * wide, wide)], store_sem.at[CHUNKS + c]
        )
        store.start()
        out_stores.append(store)

    for copy in sq_copies:
        copy.wait_send()

    for c in range(CHUNKS):

        def sent(target, _, c=c):
            state_copy(c, target).wait_send()
            return 0

        lax.fori_loop(me + 1, n, sent, 0)

    @pl.when(has_next)
    def _():
        for copy in k_copies + t_copies + v_copies:
            copy.wait_send()

    for store in mixed_stores + out_stores:
        store.wait()


def on_device(
    n,
    mp,
    stream,
    norm_gain,
    short_outer,
    short_inner,
    short_filter,
    long_outer,
    long_inner,
    long_decay,
    query_heads,
    key_heads,
):
    rows, width = stream.shape
    wide = width // CHUNKS
    forward, inverse = dft_matrices(rows)
    bf16, f32 = jnp.bfloat16, jnp.float32
    anywhere = pl.BlockSpec(memory_space=pl.ANY)
    vmem = pl.BlockSpec(memory_space=pltpu.VMEM)
    dma = pltpu.SemaphoreType.DMA
    return pl.pallas_call(
        functools.partial(kernel, n, mp, float(width * mp)),
        out_shape=[jax.ShapeDtypeStruct((rows, width), bf16)] * 2,
        in_specs=[vmem] * 2 + [anywhere] * 10,
        out_specs=[anywhere] * 2,
        scratch_shapes=[pltpu.VMEM((rows, width), bf16)] * 7
        + [
            pltpu.VMEM((2 * rows, 2 * rows), bf16),
            pltpu.VMEM((rows, 2 * rows), bf16),
        ]
        + [pltpu.VMEM((CHUNKS, 2 * rows, wide), bf16)] * 3
        + [pltpu.VMEM((rows, width), f32)] * 3
        + [
            pltpu.VMEM((2 * rows, width), f32),
            pltpu.VMEM((CHUNKS, wide // HEAD_DIM, rows, 2 * rows), bf16),
            pltpu.VMEM((CHUNKS, rows, wide), bf16),
            pltpu.VMEM((rows, 128), f32),
            pltpu.VMEM((mp - 1, rows, 128), f32),
            pltpu.VMEM((CHUNKS, 1, wide), f32),
            pltpu.VMEM((CHUNKS, n, 1, wide), f32),
            dma((9,)),
            dma((CHUNKS,)),
            dma((2 * CHUNKS,)),
            dma((mp - 1,)),
            dma((mp - 1,)),
        ]
        + [dma((CHUNKS,))] * 6
        + [dma((CHUNKS, n))] * 2,
        compiler_params=pltpu.CompilerParams(
            collective_id=0, has_side_effects=True, vmem_limit_bytes=60 * 1024 * 1024
        ),
    )(
        norm_gain.reshape(1, width),
        long_decay.reshape(1, width),
        stream,
        short_outer,
        short_inner,
        short_filter,
        long_outer,
        long_inner,
        query_heads,
        key_heads,
        jnp.asarray(forward, bf16),
        jnp.asarray(inverse, bf16),
    )


def solution(mesh):
    return jax.shard_map(
        functools.partial(on_device, mesh.shape["seq"], mesh.shape["mp"]),
        mesh=mesh,
        in_specs=(
            P("seq", "mp"),
            P("mp"),
            P("seq", "mp"),
            P("seq", "mp"),
            P(None, "mp"),
            P("seq", "mp"),
            P("seq", "mp"),
            P("mp"),
            P("seq", "mp"),
            P("seq", "mp"),
        ),
        out_specs=(P("seq", "mp"), P("seq", "mp")),
        check_vma=False,
    )
```

time: 250 us -> 53.2 us (0.21)
  the two profiles are of different devices: /device:TPU:1 before, /device:TPU:16 now
where the time goes in v1:
time: 53.2 us; the launch traced here: 52.8 us
  Pallas kernels  48.8 us (92%)
  local copies, waits for them, and re-layouts  3.35 us (6%)
  between operations  0.65 us (1%)
    pallas_call x1, Pallas kernels, on_device(): pl.pallas_call(functools.partial(kernel, n, mp, float(width * mp)), out_s...  48.8 us
    unnamed x4, local copies, waits for them, and re-layouts  3.35 us

profile of v1, /device:TPU:16, one launch (start us, length us, event | category | flops | bytes accessed | tf_op | source)
XLA Modules:
  0.0 52.8 jit_solution(8437557856735506911)
XLA Ops:
  0.6 48.8 %shard_map.131 = (bf16[128,4096]{1,0:T(8,128)(2,1)}, bf16[128,4096]{1,0:T(8,128)(2,1)}) custom-call(f32[1,4096]{1,0:T(1,128)} %bitcast.2, f32[1,4096]{1,0:T(1,128)} %bitcast.3, bf16[128,4096]{1,0:T(8,128)(2,1)} %stream_hbm.1, bf16[128,4096]{1,0:T(8,128)(2,1)} %souter_hbm.1, bf16[128,4096]{1,0:T(8,128)(2,1)} %sinner_hbm.1, bf16[128,4096]{1,0:T(8,128)(2,1)} %filt_hbm.1, ...), custom_call_target="tpu_custom_call" | custom-call | tf_op jit(solution)/shard_map/pallas_call | solution.py:413
  49.5 0.0 copy-start
  49.5 2.4 %copy.16 = bf16[128,4096]{1,0:T(8,128)(2,1)} copy(bf16[128,4096]{1,0:T(8,128)(2,1)} %get-tuple-element.4) | data formatting | bytes 2097152
  51.9 0.0 copy-done
  51.9 1.0 %copy.17 = bf16[128,4096]{1,0:T(8,128)(2,1)} copy(bf16[128,4096]{1,0:T(8,128)(2,1)S(1)} %copy-done) | data formatting | bytes 2097152
Async XLA Ops:
  49.5 2.4 %copy-start = (bf16[128,4096]{1,0:T(8,128)(2,1)S(1)}, bf16[128,4096]{1,0:T(8,128)(2,1)}, u32[]{:S(2)}) copy-start(bf16[128,4096]{1,0:T(8,128)(2,1)} %get-tuple-element.5) | copy-start | bytes 3145732

commit v2 on v1

--- a/solution.py
+++ b/solution.py
@@ -10,18 +10,15 @@
 
 HEAD_DIM = 128
 CHUNKS = 4
+PAIR = 2
 TILE = 256
 MESH = pl.DeviceIdType.MESH
 
 
-def dft_matrices(rows):
-    size = 2 * rows
-    theta = 2.0 * np.pi * (np.arange(rows) + 0.5) / size
-    angle = theta[:, None] * np.arange(size)[None, :]
-    forward = np.concatenate([np.cos(angle), -np.sin(angle)], axis=0)
-    late = angle[:, rows:].T
-    inverse = np.concatenate([np.cos(late), -np.sin(late)], axis=1) / rows
-    return forward, inverse
+def wave(frequency, place, rows):
+    shift = jnp.where(frequency >= rows, rows, 0)
+    index = lax.rem((2 * lax.rem(frequency, rows) + 1) * place + shift, 4 * rows)
+    return jnp.cos(index.astype(jnp.float32) * (np.pi / (2 * rows)))
 
 
 def dot(a, b):
@@ -42,10 +39,8 @@
     linner_hbm,
     query_hbm,
     key_hbm,
-    fwd_hbm,
-    inv_hbm,
-    mixed_hbm,
-    attended_hbm,
+    mixed,
+    attended,
     stream,
     souter,
     sinner,
@@ -63,14 +58,16 @@
     cum,
     spectrum,
     weights,
-    attended,
     squares,
     squares_in,
     own_state,
+    pair_state,
+    group_state,
+    next_state,
+    carry_in,
     states,
     load_sem,
     key_sem,
-    store_sem,
     sq_send,
     sq_recv,
     k_send,
@@ -79,6 +76,10 @@
     t_recv,
     v_send,
     v_recv,
+    p_send,
+    p_recv,
+    q_send,
+    q_recv,
     e_send,
     e_recv,
 ):
@@ -90,18 +91,34 @@
     heads = wide // HEAD_DIM
     has_next = me < n - 1
     has_prev = me > 0
+    groups = n // PAIR
+    group = me // PAIR
+    leads = lax.rem(me, PAIR) == 0
+    follows = lax.rem(me, PAIR) != 0
     own = pl.ds(rows, rows)
     before = pl.ds(0, rows)
 
     barrier = pltpu.get_barrier_semaphore()
 
-    def greet(k, _):
-        pl.semaphore_signal(
-            barrier, inc=1, device_id={"seq": lax.rem(me + k, n)}, device_id_type=MESH
-        )
-        return 0
-
-    lax.fori_loop(1, n, greet, 0)
+    def greet(target):
+        pl.semaphore_signal(barrier, inc=1, device_id={"seq": target}, device_id_type=MESH)
+
+    @pl.when(has_next)
+    def _():
+        greet(me + 1)
+
+    @pl.when(has_prev)
+    def _():
+        greet(me - 1)
+
+    @pl.when(leads)
+    def _():
+        def greet_leader(k, _):
+            greet(lax.rem(me + PAIR * k, n))
+            return 0
+
+        lax.fori_loop(1, groups, greet_leader, 0)
+
     for k in range(1, mp):
         pl.semaphore_signal(
             barrier, inc=1, device_id={"mp": lax.rem(col + k, mp)}, device_id_type=MESH
@@ -109,10 +126,8 @@
 
     pairs = [
         (stream_hbm, stream),
-        (fwd_hbm, fwd),
         (filt_hbm, filt),
         (sinner_hbm, sinner),
-        (inv_hbm, inv),
         (souter_hbm, souter),
         (linner_hbm, linner),
         (louter_hbm, louter),
@@ -162,7 +177,8 @@
     squares[...] = lax.fori_loop(
         0, width // 128, square, jnp.zeros((rows, 128), jnp.float32), unroll=4
     )
-    pl.semaphore_wait(barrier, n - 1 + mp - 1)
+    greeted = has_next.astype(jnp.int32) + has_prev.astype(jnp.int32) + mp - 1
+    pl.semaphore_wait(barrier, jnp.where(leads, greeted + groups - 1, greeted))
     sq_copies = [
         pltpu.make_async_remote_copy(
             src_ref=squares,
@@ -182,8 +198,22 @@
     def _():
         k_copies[0].start()
 
-    for copy in loads[1:4]:
+    for copy in loads[1:3]:
         copy.wait()
+
+    full = (2 * rows, 2 * rows)
+    fwd[...] = wave(
+        lax.broadcasted_iota(jnp.int32, full, 0), lax.broadcasted_iota(jnp.int32, full, 1), rows
+    ).astype(jnp.bfloat16)
+    half = (rows, 2 * rows)
+    inv[...] = (
+        wave(
+            lax.broadcasted_iota(jnp.int32, half, 1),
+            lax.broadcasted_iota(jnp.int32, half, 0) + rows,
+            rows,
+        )
+        / rows
+    ).astype(jnp.bfloat16)
 
     def spectra(i, _):
         cols = pl.ds(pl.multiple_of(i * TILE, TILE), TILE)
@@ -215,6 +245,14 @@
         def _(c=c):
             t_copies[c].start()
 
+    for copy in key_loads[1:]:
+        copy.wait()
+
+    @pl.when(has_next)
+    def _():
+        for c in range(1, CHUNKS):
+            k_copies[c].start()
+
     step = lax.broadcasted_iota(jnp.int32, (rows, TILE), 0).astype(jnp.float32)
 
     def powers(i, _):
@@ -225,7 +263,7 @@
         return 0
 
     lax.fori_loop(0, width // TILE, powers, 0)
-    for copy in loads[4:]:
+    for copy in loads[3:]:
         copy.wait()
     row = lax.broadcasted_iota(jnp.int32, (rows, 2 * rows), 0)
     column = lax.broadcasted_iota(jnp.int32, (rows, 2 * rows), 1)
@@ -235,13 +273,36 @@
 
     def state_copy(c, target):
         return pltpu.make_async_remote_copy(
+            src_ref=group_state.at[c],
+            dst_ref=states.at[c, group],
+            send_sem=e_send.at[c, target],
+            recv_sem=e_recv.at[c, group],
+            device_id={"seq": lax.rem(target * PAIR, n)},
+            device_id_type=MESH,
+        )
+
+    p_copies = [
+        pltpu.make_async_remote_copy(
             src_ref=own_state.at[c],
-            dst_ref=states.at[c, me],
-            send_sem=e_send.at[c, target],
-            recv_sem=e_recv.at[c, me],
-            device_id={"seq": target},
+            dst_ref=pair_state.at[c],
+            send_sem=p_send.at[c],
+            recv_sem=p_recv.at[c],
+            device_id={"seq": lax.rem(me + n - 1, n)},
             device_id_type=MESH,
         )
+        for c in range(CHUNKS)
+    ]
+    q_copies = [
+        pltpu.make_async_remote_copy(
+            src_ref=next_state.at[c],
+            dst_ref=carry_in.at[c],
+            send_sem=q_send.at[c],
+            recv_sem=q_recv.at[c],
+            device_id={"seq": lax.rem(me + 1, n)},
+            device_id_type=MESH,
+        )
+        for c in range(CHUNKS)
+    ]
 
     for c in range(CHUNKS):
 
@@ -272,38 +333,51 @@
 
         lax.fori_loop(0, tiles, mix, 0)
 
-        def send_state(target, _, c=c):
-            state_copy(c, target).start()
-            return 0
-
-        lax.fori_loop(me + 1, n, send_state, 0)
-
-    for copy in key_loads[1:]:
-        copy.wait()
-
-    @pl.when(has_next)
-    def _():
-        for c in range(1, CHUNKS):
-            k_copies[c].start()
-
-    mixed_stores = []
+        @pl.when(follows)
+        def _(c=c):
+            p_copies[c].start()
+
+        @pl.when(leads)
+        def _(c=c):
+            p_copies[c].wait_recv()
+            rate = decay_ref[:, pl.ds(c * wide, wide)]
+            group_state[c] = own_state[c] * jnp.exp(-rate * rows) + pair_state[c]
+
+            def send_state(target, _, c=c):
+                state_copy(c, target).start()
+                return 0
+
+            lax.fori_loop(group + 1, groups, send_state, 0)
+
     for c in range(CHUNKS):
         chunk = pl.ds(c * wide, wide)
         rate = decay_ref[:, chunk]
-        over_block = jnp.exp(-rate * rows)
-
-        def arrive(j, state, c=c, over_block=over_block):
-            pltpu.make_async_remote_copy(
-                src_ref=own_state.at[c],
-                dst_ref=states.at[c, j],
-                send_sem=e_send.at[c, me],
-                recv_sem=e_recv.at[c, j],
-                device_id={"seq": j},
-                device_id_type=MESH,
-            ).wait_recv()
-            return state * over_block + states[c, j]
-
-        carried = lax.fori_loop(0, me, arrive, jnp.zeros((1, wide), jnp.float32))
+
+        @pl.when(leads)
+        def _(c=c, rate=rate):
+            over_group = jnp.exp(-rate * (rows * PAIR))
+
+            def arrive(j, state):
+                pltpu.make_async_remote_copy(
+                    src_ref=group_state.at[c],
+                    dst_ref=states.at[c, j],
+                    send_sem=e_send.at[c, group],
+                    recv_sem=e_recv.at[c, j],
+                    device_id={"seq": j * PAIR},
+                    device_id_type=MESH,
+                ).wait_recv()
+                return state * over_group + states[c, j]
+
+            state = lax.fori_loop(0, group, arrive, jnp.zeros((1, wide), jnp.float32))
+            next_state[c] = state * jnp.exp(-rate * rows) + own_state[c]
+            q_copies[c].start()
+            carry_in[c] = state
+
+        @pl.when(follows)
+        def _(c=c):
+            q_copies[c].wait_recv()
+
+        carried = carry_in[c]
         carried = carried * jnp.exp(-rate)
         z = 2.0 * rate
         scale = jnp.sqrt(jnp.tanh(0.5 * z) * (1.0 + jnp.exp(-z)))
@@ -312,19 +386,15 @@
             cols = pl.ds(c * wide + i * TILE, TILE)
             part = slice(i * TILE, (i + 1) * TILE)
             conv = (cum[:, cols] + carried[:, part]) * power[:, cols]
-            values[c, own, here] = (
+            out = (
                 louter[:, cols].astype(jnp.float32) * (conv * scale[:, part])
             ).astype(jnp.bfloat16)
+            values[c, own, here] = out
+            mixed[:, cols] = out
 
         @pl.when(has_next)
         def _(c=c):
             v_copies[c].start()
-
-        store = pltpu.make_async_copy(
-            values.at[c, own], mixed_hbm.at[:, chunk], store_sem.at[c]
-        )
-        store.start()
-        mixed_stores.append(store)
 
     valid = (column <= row + rows) & ((column >= rows) | has_prev)
     for c in range(CHUNKS):
@@ -350,7 +420,6 @@
 
         lax.fori_loop(0, heads, score, 0, unroll=2)
 
-    out_stores = []
     for c in range(CHUNKS):
 
         @pl.when(has_prev)
@@ -359,34 +428,35 @@
 
         def gather(h, _, c=c):
             here = pl.ds(pl.multiple_of(h * HEAD_DIM, HEAD_DIM), HEAD_DIM)
-            attended[c, :, here] = dot(weights[c, h], values[c, :, here]).astype(jnp.bfloat16)
+            cols = pl.ds(pl.multiple_of(c * wide + h * HEAD_DIM, HEAD_DIM), HEAD_DIM)
+            attended[:, cols] = dot(weights[c, h], values[c, :, here]).astype(jnp.bfloat16)
             return 0
 
         lax.fori_loop(0, heads, gather, 0, unroll=2)
-        store = pltpu.make_async_copy(
-            attended.at[c], attended_hbm.at[:, pl.ds(c * wide, wide)], store_sem.at[CHUNKS + c]
-        )
-        store.start()
-        out_stores.append(store)
 
     for copy in sq_copies:
         copy.wait_send()
 
     for c in range(CHUNKS):
 
-        def sent(target, _, c=c):
-            state_copy(c, target).wait_send()
-            return 0
-
-        lax.fori_loop(me + 1, n, sent, 0)
+        @pl.when(follows)
+        def _(c=c):
+            p_copies[c].wait_send()
+
+        @pl.when(leads)
+        def _(c=c):
+            q_copies[c].wait_send()
+
+            def sent(target, _):
+                state_copy(c, target).wait_send()
+                return 0
+
+            lax.fori_loop(group + 1, groups, sent, 0)
 
     @pl.when(has_next)
     def _():
         for copy in k_copies + t_copies + v_copies:
             copy.wait_send()
-
-    for store in mixed_stores + out_stores:
-        store.wait()
 
 
 def on_device(
@@ -405,16 +475,15 @@
 ):
     rows, width = stream.shape
     wide = width // CHUNKS
-    forward, inverse = dft_matrices(rows)
     bf16, f32 = jnp.bfloat16, jnp.float32
-    anywhere = pl.BlockSpec(memory_space=pl.ANY)
+    anywhere = pl.BlockSpec(memory_space=pltpu.HBM)
     vmem = pl.BlockSpec(memory_space=pltpu.VMEM)
     dma = pltpu.SemaphoreType.DMA
     return pl.pallas_call(
         functools.partial(kernel, n, mp, float(width * mp)),
         out_shape=[jax.ShapeDtypeStruct((rows, width), bf16)] * 2,
-        in_specs=[vmem] * 2 + [anywhere] * 10,
-        out_specs=[anywhere] * 2,
+        in_specs=[vmem] * 2 + [anywhere] * 8,
+        out_specs=[vmem] * 2,
         scratch_shapes=[pltpu.VMEM((rows, width), bf16)] * 7
         + [
             pltpu.VMEM((2 * rows, 2 * rows), bf16),
@@ -425,21 +494,21 @@
         + [
             pltpu.VMEM((2 * rows, width), f32),
             pltpu.VMEM((CHUNKS, wide // HEAD_DIM, rows, 2 * rows), bf16),
-            pltpu.VMEM((CHUNKS, rows, wide), bf16),
             pltpu.VMEM((rows, 128), f32),
             pltpu.VMEM((mp - 1, rows, 128), f32),
-            pltpu.VMEM((CHUNKS, 1, wide), f32),
-            pltpu.VMEM((CHUNKS, n, 1, wide), f32),
-            dma((9,)),
+        ]
+        + [pltpu.VMEM((CHUNKS, 1, wide), f32)] * 5
+        + [
+            pltpu.VMEM((CHUNKS, n // PAIR, 1, wide), f32),
+            dma((7,)),
             dma((CHUNKS,)),
-            dma((2 * CHUNKS,)),
             dma((mp - 1,)),
             dma((mp - 1,)),
         ]
-        + [dma((CHUNKS,))] * 6
-        + [dma((CHUNKS, n))] * 2,
+        + [dma((CHUNKS,))] * 10
+        + [dma((CHUNKS, n // PAIR))] * 2,
         compiler_params=pltpu.CompilerParams(
-            collective_id=0, has_side_effects=True, vmem_limit_bytes=60 * 1024 * 1024
+            collective_id=0, has_side_effects=True, vmem_limit_bytes=51 * 1024 * 1024
         ),
     )(
         norm_gain.reshape(1, width),
@@ -452,8 +521,6 @@
         long_inner,
         query_heads,
         key_heads,
-        jnp.asarray(forward, bf16),
-        jnp.asarray(inverse, bf16),
     )
 
 

time: 53.2 us -> 47.1 us (0.89)
  Pallas kernels: 48.8 us -> 42.7 us
    pallas_call x1, Pallas kernels: 48.8 us -> 42.7 us  [on_device(): pl.pallas_call(functools.partial(kernel, n, mp, float(width * mp)), out_s...]
    unnamed x4 -> x6, local copies, waits for them, and re-layouts: 3.35 us -> 3.37 us
where the time goes in v2:
time: 47.1 us; the launch traced here: 46.7 us
  Pallas kernels  42.7 us (91%)
  local copies, waits for them, and re-layouts  3.37 us (7%)
  between operations  0.65 us (1%)
    pallas_call x1, Pallas kernels, on_device(): pl.pallas_call(functools.partial(kernel, n, mp, float(width * mp)), out_s...  42.7 us
    unnamed x6, local copies, waits for them, and re-layouts  3.37 us

profile of v2, /device:TPU:16, one launch (start us, length us, event | category | flops | bytes accessed | tf_op | source)
XLA Modules:
  0.0 46.7 jit_solution(10360354428062988085)
XLA Ops:
  0.6 0.0 copy-start
  0.6 0.7 %copy-done = f32[4096]{0:T(1024)S(1)} copy-done((f32[4096]{0:T(1024)S(1)}, f32[4096]{0:T(1024)}, u32[]{:S(2)}) %copy-start) | copy-done | bytes 16408
  1.4 0.0 copy-start.1
  1.4 0.7 %copy-done.1 = f32[4096]{0:T(1024)S(1)} copy-done((f32[4096]{0:T(1024)S(1)}, f32[4096]{0:T(1024)}, u32[]{:S(2)}) %copy-start.1) | copy-done | bytes 16408
  2.1 42.7 %shard_map.113 = (bf16[128,4096]{1,0:T(8,128)(2,1)S(1)}, bf16[128,4096]{1,0:T(8,128)(2,1)S(1)}) custom-call(f32[1,4096]{1,0:T(1,128)S(1)} %bitcast.2, f32[1,4096]{1,0:T(1,128)S(1)} %bitcast.3, bf16[128,4096]{1,0:T(8,128)(2,1)} %stream_hbm.1, bf16[128,4096]{1,0:T(8,128)(2,1)} %souter_hbm.1, bf16[128,4096]{1,0:T(8,128)(2,1)} %sinner_hbm.1, ...), custom_call_target="tpu_custom_call" | custom-call | tf_op jit(solution)/shard_map/pallas_call | solution.py:482
  44.8 1.0 %copy.14 = bf16[128,4096]{1,0:T(8,128)(2,1)} copy(bf16[128,4096]{1,0:T(8,128)(2,1)S(1)} %get-tuple-element.4) | data formatting | bytes 2097152
  45.8 1.0 %copy.15 = bf16[128,4096]{1,0:T(8,128)(2,1)} copy(bf16[128,4096]{1,0:T(8,128)(2,1)S(1)} %get-tuple-element.5) | data formatting | bytes 2097152
Async XLA Ops:
  0.6 0.7 %copy-start = (f32[4096]{0:T(1024)S(1)}, f32[4096]{0:T(1024)}, u32[]{:S(2)}) copy-start(f32[4096]{0:T(1024)} %param.11) | copy-start | bytes 49156
  1.4 0.7 %copy-start.1 = (f32[4096]{0:T(1024)S(1)}, f32[4096]{0:T(1024)}, u32[]{:S(2)}) copy-start(f32[4096]{0:T(1024)} %param.17) | copy-start | bytes 49156

commit v3 on v2

--- a/solution.py
+++ b/solution.py
@@ -11,6 +11,7 @@
 HEAD_DIM = 128
 CHUNKS = 4
 PAIR = 2
+EARLY = 2
 TILE = 256
 MESH = pl.DeviceIdType.MESH
 
@@ -29,8 +30,8 @@
     n,
     mp,
     channels,
-    gain_ref,
-    decay_ref,
+    gain_hbm,
+    decay_hbm,
     stream_hbm,
     souter_hbm,
     sinner_hbm,
@@ -41,6 +42,8 @@
     key_hbm,
     mixed,
     attended,
+    gain_ref,
+    decay_ref,
     stream,
     souter,
     sinner,
@@ -132,6 +135,8 @@
         (linner_hbm, linner),
         (louter_hbm, louter),
         (query_hbm, query),
+        (gain_hbm, gain_ref),
+        (decay_hbm, decay_ref),
     ]
     loads = [pltpu.make_async_copy(s, d, load_sem.at[i]) for i, (s, d) in enumerate(pairs)]
     key_loads = [
@@ -140,11 +145,12 @@
         )
         for c in range(CHUNKS)
     ]
+    key_loads[0].start()
     loads[0].start()
-    key_loads[0].start()
+    key_loads[1].start()
     for copy in loads[1:]:
         copy.start()
-    for copy in key_loads[1:]:
+    for copy in key_loads[EARLY:]:
         copy.start()
 
     def to_next(buffer, c, send, recv):
@@ -168,6 +174,15 @@
             values[c, :rows, :] = jnp.zeros((rows, wide), values.dtype)
             ext[c, :rows, :] = jnp.zeros((rows, wide), ext.dtype)
 
+    greeted = has_next.astype(jnp.int32) + has_prev.astype(jnp.int32) + mp - 1
+    pl.semaphore_wait(barrier, jnp.where(leads, greeted + groups - 1, greeted))
+    for c in range(EARLY):
+        key_loads[c].wait()
+
+        @pl.when(has_next)
+        def _(c=c):
+            k_copies[c].start()
+
     loads[0].wait()
 
     def square(i, acc):
@@ -177,8 +192,6 @@
     squares[...] = lax.fori_loop(
         0, width // 128, square, jnp.zeros((rows, 128), jnp.float32), unroll=4
     )
-    greeted = has_next.astype(jnp.int32) + has_prev.astype(jnp.int32) + mp - 1
-    pl.semaphore_wait(barrier, jnp.where(leads, greeted + groups - 1, greeted))
     sq_copies = [
         pltpu.make_async_remote_copy(
             src_ref=squares,
@@ -192,13 +205,7 @@
     ]
     for copy in sq_copies:
         copy.start()
-    key_loads[0].wait()
-
-    @pl.when(has_next)
-    def _():
-        k_copies[0].start()
-
-    for copy in loads[1:3]:
+    for copy in loads[1:3] + loads[7:]:
         copy.wait()
 
     full = (2 * rows, 2 * rows)
@@ -245,12 +252,12 @@
         def _(c=c):
             t_copies[c].start()
 
-    for copy in key_loads[1:]:
+    for copy in key_loads[EARLY:]:
         copy.wait()
 
     @pl.when(has_next)
     def _():
-        for c in range(1, CHUNKS):
+        for c in range(EARLY, CHUNKS):
             k_copies[c].start()
 
     step = lax.broadcasted_iota(jnp.int32, (rows, TILE), 0).astype(jnp.float32)
@@ -263,7 +270,7 @@
         return 0
 
     lax.fori_loop(0, width // TILE, powers, 0)
-    for copy in loads[3:]:
+    for copy in loads[3:7]:
         copy.wait()
     row = lax.broadcasted_iota(jnp.int32, (rows, 2 * rows), 0)
     column = lax.broadcasted_iota(jnp.int32, (rows, 2 * rows), 1)
@@ -432,7 +439,7 @@
             attended[:, cols] = dot(weights[c, h], values[c, :, here]).astype(jnp.bfloat16)
             return 0
 
-        lax.fori_loop(0, heads, gather, 0, unroll=2)
+        lax.fori_loop(0, heads, gather, 0, unroll=8)
 
     for copy in sq_copies:
         copy.wait_send()
@@ -482,9 +489,10 @@
     return pl.pallas_call(
         functools.partial(kernel, n, mp, float(width * mp)),
         out_shape=[jax.ShapeDtypeStruct((rows, width), bf16)] * 2,
-        in_specs=[vmem] * 2 + [anywhere] * 8,
+        in_specs=[anywhere] * 10,
         out_specs=[vmem] * 2,
-        scratch_shapes=[pltpu.VMEM((rows, width), bf16)] * 7
+        scratch_shapes=[pltpu.VMEM((1, width), f32)] * 2
+        + [pltpu.VMEM((rows, width), bf16)] * 7
         + [
             pltpu.VMEM((2 * rows, 2 * rows), bf16),
             pltpu.VMEM((rows, 2 * rows), bf16),
@@ -500,7 +508,7 @@
         + [pltpu.VMEM((CHUNKS, 1, wide), f32)] * 5
         + [
             pltpu.VMEM((CHUNKS, n // PAIR, 1, wide), f32),
-            dma((7,)),
+            dma((9,)),
             dma((CHUNKS,)),
             dma((mp - 1,)),
             dma((mp - 1,)),

time: 47.1 us -> 45.6 us (0.968)
  Pallas kernels: 42.7 us -> 41.2 us
    pallas_call x1, Pallas kernels: 42.7 us -> 41.2 us  [on_device(): pl.pallas_call(functools.partial(kernel, n, mp, float(width * mp)), out_s...]
where the time goes in v3:
time: 45.6 us; the launch traced here: 45.2 us
  Pallas kernels  41.2 us (90%)
  local copies, waits for them, and re-layouts  3.37 us (7%)
  between operations  0.65 us (1%)
    pallas_call x1, Pallas kernels, on_device(): pl.pallas_call(functools.partial(kernel, n, mp, float(width * mp)), out_s...  41.2 us
    unnamed x6, local copies, waits for them, and re-layouts  3.37 us

profile of v3, /device:TPU:16, one launch (start us, length us, event | category | flops | bytes accessed | tf_op | source)
XLA Modules:
  0.0 45.2 jit_solution(12049901443920071067)
XLA Ops:
  0.6 0.0 copy-start
  0.6 0.7 %copy-done = f32[4096]{0:T(1024)S(1)} copy-done((f32[4096]{0:T(1024)S(1)}, f32[4096]{0:T(1024)}, u32[]{:S(2)}) %copy-start) | copy-done | bytes 16408
  1.4 0.0 copy-start.1
  1.4 0.7 %copy-done.1 = f32[4096]{0:T(1024)S(1)} copy-done((f32[4096]{0:T(1024)S(1)}, f32[4096]{0:T(1024)}, u32[]{:S(2)}) %copy-start.1) | copy-done | bytes 16408
  2.1 41.2 %shard_map.113 = (bf16[128,4096]{1,0:T(8,128)(2,1)S(1)}, bf16[128,4096]{1,0:T(8,128)(2,1)S(1)}) custom-call(f32[1,4096]{1,0:T(1,128)S(1)} %bitcast.2, f32[1,4096]{1,0:T(1,128)S(1)} %bitcast.3, bf16[128,4096]{1,0:T(8,128)(2,1)} %stream_hbm.1, bf16[128,4096]{1,0:T(8,128)(2,1)} %souter_hbm.1, bf16[128,4096]{1,0:T(8,128)(2,1)} %sinner_hbm.1, ...), custom_call_target="tpu_custom_call" | custom-call | tf_op jit(solution)/shard_map/pallas_call | solution.py:489
  43.3 1.0 %copy.14 = bf16[128,4096]{1,0:T(8,128)(2,1)} copy(bf16[128,4096]{1,0:T(8,128)(2,1)S(1)} %get-tuple-element.4) | data formatting | bytes 2097152
  44.2 1.0 %copy.15 = bf16[128,4096]{1,0:T(8,128)(2,1)} copy(bf16[128,4096]{1,0:T(8,128)(2,1)S(1)} %get-tuple-element.5) | data formatting | bytes 2097152
Async XLA Ops:
  0.6 0.7 %copy-start = (f32[4096]{0:T(1024)S(1)}, f32[4096]{0:T(1024)}, u32[]{:S(2)}) copy-start(f32[4096]{0:T(1024)} %param.11) | copy-start | bytes 49156
  1.4 0.7 %copy-start.1 = (f32[4096]{0:T(1024)S(1)}, f32[4096]{0:T(1024)}, u32[]{:S(2)}) copy-start(f32[4096]{0:T(1024)} %param.17) | copy-start | bytes 49156

commit v4 on v3

--- a/solution.py
+++ b/solution.py
@@ -9,9 +9,9 @@
 from jax.sharding import PartitionSpec as P
 
 HEAD_DIM = 128
-CHUNKS = 4
+CHUNKS = 8
 PAIR = 2
-EARLY = 2
+EARLY = 3
 TILE = 256
 MESH = pl.DeviceIdType.MESH
 
@@ -145,9 +145,9 @@
         )
         for c in range(CHUNKS)
     ]
-    key_loads[0].start()
+    for copy in key_loads[:EARLY]:
+        copy.start()
     loads[0].start()
-    key_loads[1].start()
     for copy in loads[1:]:
         copy.start()
     for copy in key_loads[EARLY:]:
@@ -439,7 +439,7 @@
             attended[:, cols] = dot(weights[c, h], values[c, :, here]).astype(jnp.bfloat16)
             return 0
 
-        lax.fori_loop(0, heads, gather, 0, unroll=8)
+        lax.fori_loop(0, heads, gather, 0, unroll=heads)
 
     for copy in sq_copies:
         copy.wait_send()

time: 45.6 us -> 47.4 us (1.039)
  Pallas kernels: 41.2 us -> 43.1 us
    pallas_call x1, Pallas kernels: 41.2 us -> 43.1 us  [on_device(): pl.pallas_call(functools.partial(kernel, n, mp, float(width * mp)), out_s...]
where the time goes in v4:
time: 47.4 us; the launch traced here: 47.1 us
  Pallas kernels  43.1 us (91%)
  local copies, waits for them, and re-layouts  3.37 us (7%)
  between operations  0.65 us (1%)
    pallas_call x1, Pallas kernels, on_device(): pl.pallas_call(functools.partial(kernel, n, mp, float(width * mp)), out_s...  43.1 us
    unnamed x6, local copies, waits for them, and re-layouts  3.37 us

profile of v4, /device:TPU:16, one launch (start us, length us, event | category | flops | bytes accessed | tf_op | source)
XLA Modules:
  0.0 47.1 jit_solution(16159507322387794392)
XLA Ops:
  0.6 0.0 copy-start
  0.6 0.7 %copy-done = f32[4096]{0:T(1024)S(1)} copy-done((f32[4096]{0:T(1024)S(1)}, f32[4096]{0:T(1024)}, u32[]{:S(2)}) %copy-start) | copy-done | bytes 16408
  1.4 0.0 copy-start.1
  1.4 0.7 %copy-done.1 = f32[4096]{0:T(1024)S(1)} copy-done((f32[4096]{0:T(1024)S(1)}, f32[4096]{0:T(1024)}, u32[]{:S(2)}) %copy-start.1) | copy-done | bytes 16408
  2.1 43.1 %shard_map.113 = (bf16[128,4096]{1,0:T(8,128)(2,1)S(1)}, bf16[128,4096]{1,0:T(8,128)(2,1)S(1)}) custom-call(f32[1,4096]{1,0:T(1,128)S(1)} %bitcast.2, f32[1,4096]{1,0:T(1,128)S(1)} %bitcast.3, bf16[128,4096]{1,0:T(8,128)(2,1)} %stream_hbm.1, bf16[128,4096]{1,0:T(8,128)(2,1)} %souter_hbm.1, bf16[128,4096]{1,0:T(8,128)(2,1)} %sinner_hbm.1, ...), custom_call_target="tpu_custom_call" | custom-call | tf_op jit(solution)/shard_map/pallas_call | solution.py:489
  45.1 1.0 %copy.14 = bf16[128,4096]{1,0:T(8,128)(2,1)} copy(bf16[128,4096]{1,0:T(8,128)(2,1)S(1)} %get-tuple-element.4) | data formatting | bytes 2097152
  46.1 1.0 %copy.15 = bf16[128,4096]{1,0:T(8,128)(2,1)} copy(bf16[128,4096]{1,0:T(8,128)(2,1)S(1)} %get-tuple-element.5) | data formatting | bytes 2097152
Async XLA Ops:
  0.6 0.7 %copy-start = (f32[4096]{0:T(1024)S(1)}, f32[4096]{0:T(1024)}, u32[]{:S(2)}) copy-start(f32[4096]{0:T(1024)} %param.11) | copy-start | bytes 49156
  1.4 0.7 %copy-start.1 = (f32[4096]{0:T(1024)S(1)}, f32[4096]{0:T(1024)}, u32[]{:S(2)}) copy-start(f32[4096]{0:T(1024)} %param.17) | copy-start | bytes 49156

commit v5 on v3

--- a/solution.py
+++ b/solution.py
@@ -278,6 +278,33 @@
         jnp.float32
     ).astype(jnp.bfloat16)
 
+    valid = (column <= row + rows) & ((column >= rows) | has_prev)
+    def attend(c):
+
+        @pl.when(has_prev)
+        def _():
+            k_copies[c].wait_recv()
+
+        def score(h, _):
+            here = pl.ds(pl.multiple_of(h * HEAD_DIM, HEAD_DIM), HEAD_DIM)
+            cols = pl.ds(pl.multiple_of(c * wide + h * HEAD_DIM, HEAD_DIM), HEAD_DIM)
+            s = lax.dot_general(
+                query[:, cols],
+                keys[c, :, here],
+                (((1,), (1,)), ((), ())),
+                preferred_element_type=jnp.float32,
+            ) * HEAD_DIM ** (-0.5)
+            s = jnp.where(valid, s, -1e30)
+            e = jnp.exp(s - jnp.max(s, axis=1, keepdims=True))
+            e = e * (1.0 / jnp.sum(e, axis=1, keepdims=True))
+            weights[c, h] = e.astype(jnp.bfloat16)
+            return 0
+
+        lax.fori_loop(0, heads, score, 0, unroll=2)
+
+    for c in range(EARLY):
+        attend(c)
+
     def state_copy(c, target):
         return pltpu.make_async_remote_copy(
             src_ref=group_state.at[c],
@@ -403,29 +430,8 @@
         def _(c=c):
             v_copies[c].start()
 
-    valid = (column <= row + rows) & ((column >= rows) | has_prev)
-    for c in range(CHUNKS):
-
-        @pl.when(has_prev)
-        def _(c=c):
-            k_copies[c].wait_recv()
-
-        def score(h, _, c=c):
-            here = pl.ds(pl.multiple_of(h * HEAD_DIM, HEAD_DIM), HEAD_DIM)
-            cols = pl.ds(pl.multiple_of(c * wide + h * HEAD_DIM, HEAD_DIM), HEAD_DIM)
-            s = lax.dot_general(
-                query[:, cols],
-                keys[c, :, here],
-                (((1,), (1,)), ((), ())),
-                preferred_element_type=jnp.float32,
-            ) * HEAD_DIM ** (-0.5)
-            s = jnp.where(valid, s, -1e30)
-            e = jnp.exp(s - jnp.max(s, axis=1, keepdims=True))
-            e = e * (1.0 / jnp.sum(e, axis=1, keepdims=True))
-            weights[c, h] = e.astype(jnp.bfloat16)
-            return 0
-
-        lax.fori_loop(0, heads, score, 0, unroll=2)
+    for c in range(EARLY, CHUNKS):
+        attend(c)
 
     for c in range(CHUNKS):
 

time: 45.6 us -> 45.6 us (level)
  no operation moved by 1% of the time
where the time goes in v5:
time: 45.6 us; the launch traced here: 45.2 us
  Pallas kernels  41.2 us (90%)
  local copies, waits for them, and re-layouts  3.37 us (7%)
  between operations  0.65 us (1%)
    pallas_call x1, Pallas kernels, on_device(): pl.pallas_call(functools.partial(kernel, n, mp, float(width * mp)), out_s...  41.2 us
    unnamed x6, local copies, waits for them, and re-layouts  3.37 us

profile of v5, /device:TPU:16, one launch (start us, length us, event | category | flops | bytes accessed | tf_op | source)
XLA Modules:
  0.0 45.2 jit_solution(15105494806399714295)
XLA Ops:
  0.6 0.0 copy-start
  0.6 0.7 %copy-done = f32[4096]{0:T(1024)S(1)} copy-done((f32[4096]{0:T(1024)S(1)}, f32[4096]{0:T(1024)}, u32[]{:S(2)}) %copy-start) | copy-done | bytes 16408
  1.4 0.0 copy-start.1
  1.4 0.7 %copy-done.1 = f32[4096]{0:T(1024)S(1)} copy-done((f32[4096]{0:T(1024)S(1)}, f32[4096]{0:T(1024)}, u32[]{:S(2)}) %copy-start.1) | copy-done | bytes 16408
  2.1 41.2 %shard_map.113 = (bf16[128,4096]{1,0:T(8,128)(2,1)S(1)}, bf16[128,4096]{1,0:T(8,128)(2,1)S(1)}) custom-call(f32[1,4096]{1,0:T(1,128)S(1)} %bitcast.2, f32[1,4096]{1,0:T(1,128)S(1)} %bitcast.3, bf16[128,4096]{1,0:T(8,128)(2,1)} %stream_hbm.1, bf16[128,4096]{1,0:T(8,128)(2,1)} %souter_hbm.1, bf16[128,4096]{1,0:T(8,128)(2,1)} %sinner_hbm.1, ...), custom_call_target="tpu_custom_call" | custom-call | tf_op jit(solution)/shard_map/pallas_call | solution.py:495
  43.3 1.0 %copy.14 = bf16[128,4096]{1,0:T(8,128)(2,1)} copy(bf16[128,4096]{1,0:T(8,128)(2,1)S(1)} %get-tuple-element.4) | data formatting | bytes 2097152
  44.2 1.0 %copy.15 = bf16[128,4096]{1,0:T(8,128)(2,1)} copy(bf16[128,4096]{1,0:T(8,128)(2,1)S(1)} %get-tuple-element.5) | data formatting | bytes 2097152
Async XLA Ops:
  0.6 0.7 %copy-start = (f32[4096]{0:T(1024)S(1)}, f32[4096]{0:T(1024)}, u32[]{:S(2)}) copy-start(f32[4096]{0:T(1024)} %param.11) | copy-start | bytes 49156
  1.4 0.7 %copy-start.1 = (f32[4096]{0:T(1024)S(1)}, f32[4096]{0:T(1024)}, u32[]{:S(2)}) copy-start(f32[4096]{0:T(1024)} %param.17) | copy-start | bytes 49156
